TPU v7x, 32 devices: a whole 2x2x4 slice. The times are simulated.
32 devices in a mesh: section: 2 (over x), tp: 16 (over z, y, core).
Axes of the slice: x: 2, y: 2, z: 4, core: 2. Of those that a mesh axis runs over, the one named last changes fastest.
Arguments:
- states: float32 [2, 128, 4096], P('section', 'tp'), may hold values from -6 to 6
- text_embed: bfloat16 [1, 128, 4096], P(None, 'tp'), may hold values from -6 to 6
- visual_embed: bfloat16 [1, 128, 4096], P(None, 'tp'), may hold values from -6 to 6
- prefix_len: int32 [1, 4], replicated, may hold values from 1 to 31
- segment_ids: int32 [3, 128], replicated, may hold values from 0 to 3, never falling along the last dimension, each value on 1 to 64 neighbouring positions
- gain: float32 [2, 4096], P('section'), may hold values from 0.25 to 1.75
- w_query: bfloat16 [2, 4096, 2048], P('section', None, 'tp'), may hold values from -0.5625 to 0.5625
- w_keyval: bfloat16 [2, 4096, 2048], P('section', None, 'tp'), may hold values from -0.5625 to 0.5625
- w_out: bfloat16 [2, 2048, 4096], P('section', 'tp'), may hold values from -0.5 to 0.5
Outputs:
- section_out: float32 [2, 2, 128, 4096], P(None, 'section', 'tp')
All inputs are finite; a program needn't handle non-finite values.
Results may differ from a plain program's by a relative error of at most 0.028.
Values may be sent and summed in bfloat16 or wider, within the bound.
A program may use at most 64 MiB of HBM per device.

v0:
```python
import jax
import jax.numpy as jnp
from jax import lax
from jax.sharding import PartitionSpec as P

HEAD = 64
WINDOW = 2


norm_eps = 1e-05
rope_base = 500000.0


def shifted(block, axis, distance):
    devices = range(lax.axis_size(axis))
    route = [(i - distance, i) for i in devices if i - distance in devices]
    return lax.ppermute(block, axis, route)


def seg_offsets(seg_row):
    earlier = (seg_row[None, :] < seg_row[:, None]).astype(jnp.int32)
    first_pos = jnp.sum(earlier, axis=1)
    return jnp.arange(seg_row.shape[0], dtype=jnp.int32) - first_pos


def rotate(values, offsets):
    half_dim = values.shape[-1] // 2
    inv_freq = rope_base ** (-(jnp.arange(half_dim, dtype=jnp.float32) * 2.0) / values.shape[-1])
    angles = offsets.astype(jnp.float32)[:, None] * inv_freq[None, :]
    view_shape = (values.shape[0],) + (1,) * (values.ndim - 2) + (half_dim,)
    cosine = jnp.cos(angles).reshape(view_shape)
    sine_part = jnp.sin(angles).reshape(view_shape)
    front_half = values[..., :half_dim]
    back_half = values[..., half_dim:]
    return jnp.concatenate(
        [front_half * cosine - back_half * sine_part, back_half * cosine + front_half * sine_part],
        axis=-1,
    )


def rms_normed(rows, gain_row):
    scale = lax.rsqrt(jnp.mean(rows * rows, axis=-1, keepdims=True) + norm_eps)
    return rows * scale * gain_row


def body(states, text_embed, visual_embed, prefix_len, segment_ids, gain, w_query, w_keyval, w_out):
    section_pos = lax.axis_index("section")
    rank_pos = lax.axis_index("tp")
    section_count = lax.axis_size("section")
    shard_rows = states.shape[1]
    gain_row = gain[0]
    query_w = w_query[0]
    keyval_w = w_keyval[0]
    out_w = w_out[0]
    query_cols = query_w.shape[1]
    residual = states[0]
    outputs = []
    for step_num in range(WINDOW):
        if step_num > 0:
            arrived = shifted(residual.astype(jnp.bfloat16), "section", 1).astype(residual.dtype)
            batch_num = step_num - 1
            embed_seg_row = segment_ids[section_count + batch_num]
            offsets = seg_offsets(embed_seg_row)
            onehot = (
                embed_seg_row[:, None] == jnp.arange(prefix_len.shape[1], dtype=jnp.int32)[None, :]
            )
            prefix_cap = jnp.sum(jnp.where(onehot, prefix_len[batch_num][None, :], 0), axis=1)
            own_visual = lax.dynamic_slice_in_dim(
                offsets < prefix_cap, rank_pos * shard_rows, shard_rows, 0
            )
            residual = jnp.where(
                section_pos == 0,
                jnp.where(
                    own_visual[:, None], visual_embed[batch_num], text_embed[batch_num]
                ).astype(jnp.float32),
                arrived,
            )
        seg_row = lax.dynamic_index_in_dim(
            segment_ids, step_num - section_pos + section_count - 1, 0, keepdims=False
        )
        apply_normed = rms_normed(residual, gain_row).astype(jnp.bfloat16)
        normed = lax.all_gather(apply_normed, "tp", axis=0, tiled=True)
        mapped = jnp.concatenate(
            [
                jnp.dot(normed, query_w, preferred_element_type=jnp.float32),
                jnp.dot(normed, keyval_w, preferred_element_type=jnp.float32),
            ],
            axis=1,
        )
        total_rows = mapped.shape[0]
        apply_offsets = seg_offsets(seg_row)
        queries = rotate(
            mapped[:, :query_cols].reshape(total_rows, query_cols // HEAD, HEAD), apply_offsets
        ).astype(jnp.bfloat16)
        key_rows = rotate(mapped[:, query_cols : query_cols + HEAD], apply_offsets).astype(
            jnp.bfloat16
        )
        value_rows = mapped[:, query_cols + HEAD :].astype(jnp.bfloat16)
        scores = jnp.einsum(
            "qhd,kd->hqk", queries, key_rows, preferred_element_type=jnp.float32
        ) * HEAD ** (-0.5)
        position = jnp.arange(total_rows, dtype=jnp.int32)
        allowed = (seg_row[None, :] == seg_row[:, None]) & (position[None, :] <= position[:, None])
        scores = jnp.where(allowed[None], scores, -1e30)
        weights = jax.nn.softmax(scores, axis=-1).astype(jnp.bfloat16)
        mixed_heads = (
            jnp.einsum("hqk,kd->qhd", weights, value_rows, preferred_element_type=jnp.float32)
            .astype(jnp.bfloat16)
            .reshape(total_rows, query_cols)
        )
        residual = residual + lax.psum_scatter(
            jnp.dot(mixed_heads, out_w, preferred_element_type=jnp.float32).astype(jnp.bfloat16),
            "tp",
            scatter_dimension=0,
            tiled=True,
        ).astype(jnp.float32)
        outputs.append(residual)
    return jnp.stack(outputs)[:, None]


def solution(mesh):
    return jax.shard_map(
        body,
        mesh=mesh,
        in_specs=(
            P("section", "tp", None),
            P(None, "tp", None),
            P(None, "tp", None),
            P(),
            P(),
            P("section", None),
            P("section", None, "tp"),
            P("section", None, "tp"),
            P("section", "tp", None),
        ),
        out_specs=P(None, "section", "tp", None),
        check_vma=False,
    )
```

profile of v0, /device:TPU:6, one launch (start us, length us, event | category | flops | bytes accessed | tf_op | source)
XLA Modules:
  0.0 225.3 jit_solution(10462846901884635893)
XLA Ops:
  6.5 1.1 fusion.20
  7.7 1.6 fusion.22
  9.4 1.6 copy.19
  11.0 0.6 slice_bitcast_fusion
  11.8 35.7 %all-gather.3.cloned.1.call-done = bf16[128,4096]{1,0:T(8,128)(2,1)} async-done(((bf16[8,4096]{1,0:T(8,128)(2,1)}), bf16[128,4096]{1,0:T(8,128)(2,1)}) %all-gather.3.cloned.1.call-update) | async-done | bytes 1048592 | tf_op jit(solution)/shard_map/all_gather | solution.py:82
  47.5 1.8 fusion.18
  50.8 1.4 convolution_convert_fusion.1
  52.3 0.6 copy-done.11
  52.9 0.7 convert_reduce_fusion.1
  53.6 0.7 select_reduce_fusion
  54.2 55.7 %reduce-scatter.3.cloned.1.call-done = bf16[8,4096]{1,0:T(8,128)(2,1)} async-done(((bf16[128,4096]{1,0:T(8,128)(2,1)}), bf16[8,4096]{1,0:T(8,128)(2,1)}) %reduce-scatter.3.cloned.1.call-update) | async-done | bytes 65552 | tf_op jit(solution)/shard_map/reduce_scatter | solution.py:111
  109.9 1.5 fusion.24
  111.4 1.3 collective-permute-start
  112.7 0.7 subtract_compare_fusion
  113.4 4.3 %collective-permute-done = bf16[8,4096]{1,0:T(8,128)(2,1)S(1)} collective-permute-done((bf16[8,4096]{1,0:T(8,128)(2,1)}, bf16[8,4096]{1,0:T(8,128)(2,1)S(1)}, u32[]{:S(2)}, u32[]{:S(2)}) %collective-permute-start) | collective-permute-done | bytes 65568 | tf_op jit(solution)/shard_map/ppermute | solution.py:17
  118.0 0.7 multiply_convert_fusion
  118.8 0.8 convert_reduce_fusion
  119.6 0.8 fusion.25
  120.5 34.4 %all-gather.5.cloned.1.call-done = bf16[128,4096]{1,0:T(8,128)(2,1)} async-done(((bf16[8,4096]{1,0:T(8,128)(2,1)}), bf16[128,4096]{1,0:T(8,128)(2,1)}) %all-gather.5.cloned.1.call-update) | async-done | bytes 1048592 | tf_op jit(solution)/shard_map/all_gather | solution.py:82
  154.9 1.8 fusion.16
  158.1 1.5 convolution_convert_fusion
  159.5 57.6 %reduce-scatter.5.cloned.1.call-done = bf16[8,4096]{1,0:T(8,128)(2,1)} async-done(((bf16[128,4096]{1,0:T(8,128)(2,1)}), bf16[8,4096]{1,0:T(8,128)(2,1)}) %reduce-scatter.5.cloned.1.call-update) | async-done | bytes 65552 | tf_op jit(solution)/shard_map/reduce_scatter | solution.py:111
  217.1 0.9 add_bitcast_fusion
  218.0 0.7 maximum_bitcast_fusion
  (54 shorter events, 3.4 us)
Async XLA Ops:
  6.5 44.2 %copy-start = (bf16[1,128,4096]{2,1,0:T(8,128)(2,1)S(1)}, bf16[1,128,4096]{2,1,0:T(8,128)(2,1)}, u32[]{:S(2)}) copy-start(bf16[1,128,4096]{2,1,0:T(8,128)(2,1)} %param.17) | copy-start | bytes 3145732
  6.5 41.0 %all-gather.3.cloned.1.call-start = ((), (), s32[]{:S(2)}) async-start(), calls=%async_computation.2 | async-start | bytes 1114112 | tf_op jit(solution)/shard_map/all_gather | solution.py:82
  9.3 100.6 %reduce-scatter.3.cloned.1.call-start = ((), (), s32[]{:S(2)}) async-start(), calls=%async_computation.3 | async-start | bytes 1114112 | tf_op jit(solution)/shard_map/reduce_scatter | solution.py:111
  9.4 1.6 copy-start.10
  9.4 38.1 %copy-start.1 = (bf16[1,4096,128]{2,1,0:T(8,128)(2,1)S(1)}, bf16[1,4096,128]{2,1,0:T(8,128)(2,1)}, u32[]{:S(2)}) copy-start(bf16[1,4096,128]{2,1,0:T(8,128)(2,1)} %param.16) | copy-start | bytes 3145732
  11.0 38.4 %copy-start.8 = (f32[32]{0:T(128)}, f32[32]{0:T(128)S(1)}, u32[]{:S(2)}) copy-start(f32[32]{0:T(128)S(1)} %multiply_power_fusion) | copy-start | bytes 388
  47.5 2.0 copy-start.2
  52.2 0.7 copy-start.11
  52.2 1.4 copy-start.12
  52.2 57.7 %copy-start.4 = (f32[1,8,4096]{2,1,0:T(8,128)S(1)}, f32[1,8,4096]{2,1,0:T(8,128)}, u32[]{:S(2)}) copy-start(f32[1,8,4096]{2,1,0:T(8,128)} %param.9) | copy-start | bytes 393220
  52.2 65.5 %copy-start.5 = (bf16[1,8,4096]{2,1,0:T(8,128)(2,1)S(1)}, bf16[1,8,4096]{2,1,0:T(8,128)(2,1)}, u32[]{:S(2)}) copy-start(bf16[1,8,4096]{2,1,0:T(8,128)(2,1)} %param.10) | copy-start | bytes 196612
  52.2 65.5 %copy-start.6 = (bf16[1,8,4096]{2,1,0:T(8,128)(2,1)S(1)}, bf16[1,8,4096]{2,1,0:T(8,128)(2,1)}, u32[]{:S(2)}) copy-start(bf16[1,8,4096]{2,1,0:T(8,128)(2,1)} %param.11) | copy-start | bytes 196612
  52.2 65.8 %copy-start.7 = (f32[1,4096]{1,0:T(1,128)S(1)}, f32[1,4096]{1,0:T(1,128)}, u32[]{:S(2)}) copy-start(f32[1,4096]{1,0:T(1,128)} %param.14) | copy-start | bytes 49156
  52.3 102.6 %all-gather.5.cloned.1.call-start = ((), (), s32[]{:S(2)}) async-start(), calls=%async_computation.4 | async-start | bytes 1114112 | tf_op jit(solution)/shard_map/all_gather | solution.py:82
  111.4 6.4 %collective-permute-start = (bf16[8,4096]{1,0:T(8,128)(2,1)}, bf16[8,4096]{1,0:T(8,128)(2,1)S(1)}, u32[]{:S(2)}, u32[]{:S(2)}) collective-permute-start(bf16[8,4096]{1,0:T(8,128)(2,1)} %get-tuple-element.8), channel_id=1, source_target_pairs={{0,16},{1,17},{2,18},{3,19},{4,20},{5,21},{6,22},{7,23},{8,24},{9,... | collective-permute-start | bytes 196616 | tf_op jit(solution)/shard_map/ppermute | solution.py:17
  118.7 98.4 %reduce-scatter.5.cloned.1.call-start = ((), (), s32[]{:S(2)}) async-start(), calls=%async_computation.5 | async-start | bytes 1114112 | tf_op jit(solution)/shard_map/reduce_scatter | solution.py:111
  120.5 36.2 %copy-start.9 = (f32[32]{0:T(128)S(1)}, f32[32]{0:T(128)}, u32[]{:S(2)}) copy-start(f32[32]{0:T(128)} %copy-done.8) | copy-start | bytes 388
  154.9 2.0 copy-start.3
Sparse Core Ops, SparseCore 0:
  9.5 37.9 all-gather.2
  52.4 57.4 reduce-scatter.2
  118.9 35.9 all-gather.4
  159.7 57.4 reduce-scatter.4
where the time goes:
time: 227 us; the launch traced here: 225 us
  waiting for transfers between devices  188 us (83%)
  between operations  13.3 us (6%)
  other arithmetic  11 us (5%)
  matrix products  8.88 us (4%)
  local copies, waits for them, and re-layouts  2.86 us (1%)
    reduce_scatter x2, waiting for transfers between devices, body(): lax.psum_scatter(jnp.dot(mixed_heads, out_w, preferred_element_type=jnp.f...  113 us
    all_gather x2, waiting for transfers between devices, body(): normed = lax.all_gather(apply_normed, 'tp', axis=0, tiled=True)  70.1 us
  transfers between devices with their start and end apart: 5, of which 5 were waited for; matrix products, arithmetic and copies ran while one was open for 3% of the time, Pallas kernels for 0%

commit v1 on v0

v1 whole, which is shorter than its diff:
```python
import functools
import math

import jax
import jax.numpy as jnp
from jax import lax
from jax.experimental import pallas as pl
from jax.experimental.pallas import tpu as pltpu
from jax.sharding import PartitionSpec as P

HEAD = 64
WINDOW = 2
NORM_EPS = 1e-05
ROPE_BASE = 500000.0
MESH = pl.DeviceIdType.MESH
F32 = jnp.float32
BF16 = jnp.bfloat16

MID = 2
INNER = 2
CHUNKS = 4


def iota(shape, dim):
    return lax.broadcasted_iota(jnp.int32, shape, dim)


def kernel(
    sections, ranks,
    states, text, visual, prefix, seg_in, gain_in, wq_in, wkv_in, wo_in,
    out,
    st_v, tx_v, vi_v, seg_v, g_v, w_v, wo_v, res, xg, xf, mix, acc,
    csend, crecv, bsend, brecv, asend, arecv, hsend, hrecv,
    load_sem, ag_send, ag_recv, c_sem, b_sem, a_send, a_recv, h_sem,
):
    s = lax.axis_index("section")
    r = lax.axis_index("tp")
    outer = ranks // (MID * INNER)
    c = lax.rem(r, INNER)
    b = lax.rem(r // INNER, MID)
    a = r // (INNER * MID)
    bp, cp = 1 - b, 1 - c
    rows = st_v.shape[0]
    depth = st_v.shape[1]
    total = rows * ranks
    qcols = wq_in.shape[2]
    kvcols = wkv_in.shape[2]
    cw = depth // CHUNKS

    def rank(ai, bi, ci):
        return (ai * MID + bi) * INNER + ci

    loads = [
        pltpu.make_async_copy(src, dst, load_sem.at[i])
        for i, (src, dst) in enumerate([
            (states.at[0], st_v),
            (gain_in, g_v),
            (seg_in, seg_v),
            (wq_in.at[0], w_v.at[:, pl.ds(0, qcols)]),
            (wkv_in.at[0], w_v.at[:, pl.ds(qcols, kvcols)]),
            (wo_in.at[0], wo_v),
            (text.at[0], tx_v),
            (visual.at[0], vi_v),
        ])
    ]
    for load in loads:
        load.start()

    outer_peers = [lax.rem(a + d, outer) for d in range(1, outer)]
    tp_peers = [rank(ai, b, c) for ai in outer_peers] + [rank(a, bp, c), rank(a, b, cp)]
    barrier = pltpu.get_barrier_semaphore()
    for peer in tp_peers:
        pl.semaphore_signal(barrier, inc=1, device_id={"tp": peer}, device_id_type=MESH)

    @pl.when(s > 0)
    def _():
        pl.semaphore_signal(barrier, inc=1, device_id={"section": s - 1}, device_id_type=MESH)

    @pl.when(s < sections - 1)
    def _():
        pl.semaphore_signal(barrier, inc=1, device_id={"section": s + 1}, device_id_type=MESH)

    loads[0].wait()
    loads[1].wait()
    loads[2].wait()

    def start_row(seg_row, seg_col):
        return jnp.sum(jnp.where(seg_row < seg_col, 1.0, 0.0), axis=1, keepdims=True)

    def column_of(seg_row, count, base):
        shape = (count, total)
        here = iota(shape, 1) == iota(shape, 0) + base
        return jnp.sum(jnp.where(here, seg_row, 0.0), axis=1, keepdims=True)

    def normed(value):
        scale = lax.rsqrt(jnp.mean(value * value, axis=-1, keepdims=True) + NORM_EPS)
        return (value * scale * g_v[...]).astype(BF16)

    sends = []

    def remote(src, dst, send_sem, recv_sem, **where):
        return pltpu.make_async_remote_copy(
            src_ref=src, dst_ref=dst, send_sem=send_sem, recv_sem=recv_sem,
            device_id=where, device_id_type=MESH,
        )

    lane = iota((total, qcols), 1)

    for t in range(WINDOW):
        if t == 0:
            res[...] = st_v[...]
        else:
            seg_row = seg_v[sections + t - 1 : sections + t, :].astype(F32)

            @pl.when(s == 0)
            def _():
                loads[6].wait()
                loads[7].wait()
                own = column_of(seg_row, rows, r * rows)
                cap = jnp.zeros_like(own)
                for d in range(prefix.shape[1]):
                    cap = cap + jnp.where(own == float(d), prefix[t - 1, d].astype(F32), 0.0)
                pos = (iota((rows, 1), 0) + r * rows).astype(F32)
                seen = pos - start_row(seg_row, own) < cap
                res[...] = jnp.where(seen, vi_v[...].astype(F32), tx_v[...].astype(F32))

            @pl.when(s > 0)
            def _():
                loads[6].wait()
                loads[7].wait()
                for k in range(CHUNKS):
                    remote(
                        hsend.at[k], hrecv.at[k], h_sem.at[0, k], h_sem.at[1, k], section=s - 1
                    ).wait_recv()
                    res[:, k * cw : (k + 1) * cw] = hrecv[k].astype(F32)

        xg[t, r] = normed(res[...])
        if t == 0:
            beside = jnp.minimum(s, 1) + jnp.minimum(sections - 1 - s, 1)
            pl.semaphore_wait(barrier, len(tp_peers) + beside)

        used = [0]

        def block(q, peer):
            copy = remote(
                xg.at[t, q], xg.at[t, q], ag_send.at[t, used[0]], ag_recv.at[t, q], tp=peer
            )
            used[0] += 1
            copy.start()
            sends.append(copy)

        def arrived(q):
            remote(
                xg.at[t, q], xg.at[t, q], ag_send.at[t, 0], ag_recv.at[t, q], tp=rank(a, b, cp)
            ).wait_recv()

        for ai in outer_peers:
            block(r, rank(ai, b, c))
        block(r, rank(a, bp, c))
        block(r, rank(a, b, cp))

        seg_here = seg_v[pl.ds(t - s + sections - 1, 1), :].astype(F32)
        seg_col = column_of(seg_here, total, 0)
        offset = iota((total, 1), 0).astype(F32) - start_row(seg_here, seg_col)
        half = HEAD // 2
        m = lax.rem(lane, half).astype(F32)
        freq = jnp.exp(m * (-2.0 / HEAD * math.log(ROPE_BASE)))
        angle = offset * freq
        cosine = jnp.cos(angle)
        front = lax.rem(lane, HEAD) < half
        sine = jnp.where(front, -jnp.sin(angle), jnp.sin(angle))
        allowed = (seg_here == seg_col) & (iota((total, total), 1) <= iota((total, total), 0))

        forward = [lax.rem(a - d + outer, outer) for d in range(1, outer)]
        for ai in forward:
            q = rank(ai, b, c)
            arrived(q)
            block(q, rank(a, bp, c))
            block(q, rank(a, b, cp))
        for ai in [a] + forward:
            q = rank(ai, bp, c)
            arrived(q)
            block(q, rank(a, b, cp))
        for ai in [a] + forward:
            for bi in (b, bp):
                arrived(rank(ai, bi, cp))

        for i in range(ranks // 2):
            xf[i * 2 * rows : (i + 1) * 2 * rows, :] = jnp.concatenate(
                [xg[t, 2 * i].astype(F32), xg[t, 2 * i + 1].astype(F32)], axis=0
            ).astype(BF16)
        if t == 0:
            loads[3].wait()
            loads[4].wait()
        mapped = jnp.dot(xf[...], w_v[...], preferred_element_type=F32)

        def rotate(value):
            swapped = jnp.where(
                front, pltpu.roll(value, qcols - half, 1), pltpu.roll(value, half, 1)
            )
            return value * cosine + swapped * sine

        queries = rotate(mapped[:, :qcols])
        keyval = mapped[:, qcols:]
        keys = rotate(keyval)
        first = lane < HEAD
        keys = jnp.where(first, keys, pltpu.roll(keys, HEAD, 1)).astype(BF16)
        values = jnp.where(first, pltpu.roll(keyval, HEAD, 1), keyval).astype(BF16)
        mixed = jnp.zeros((total, qcols), F32)
        for h in range(qcols // HEAD):
            mine = lane // HEAD == h
            scores = lax.dot_general(
                jnp.where(mine, queries, 0.0).astype(BF16), keys,
                (((1,), (1,)), ((), ())), preferred_element_type=F32,
            ) * HEAD ** (-0.5)
            scores = jnp.where(allowed, scores, -1e30)
            top = jnp.max(scores, axis=-1, keepdims=True)
            grown = jnp.exp(scores - top)
            probs = (grown / jnp.sum(grown, axis=-1, keepdims=True)).astype(BF16)
            mixed = jnp.where(mine, jnp.dot(probs, values, preferred_element_type=F32), mixed)
        for ci in range(INNER):
            mix[ci] = jnp.concatenate(
                [
                    mixed[rank(ai, bi, ci) * rows : (rank(ai, bi, ci) + 1) * rows]
                    for bi in range(MID) for ai in range(outer)
                ],
                axis=0,
            ).astype(BF16)
        if t == 0:
            loads[5].wait()

        def chunk(k):
            return slice(k * cw, (k + 1) * cw)

        def stage1(k):
            theirs = jnp.dot(mix[cp], wo_v[:, chunk(k)], preferred_element_type=F32)
            for i in range(MID * outer):
                csend[t, k, i // outer, i % outer] = theirs[i * rows : (i + 1) * rows].astype(BF16)
            copy = remote(
                csend.at[t, k], crecv.at[t, k], c_sem.at[0, t, k], c_sem.at[1, t, k],
                tp=rank(a, b, cp),
            )
            copy.start()
            sends.append(copy)
            mine = jnp.dot(mix[c], wo_v[:, chunk(k)], preferred_element_type=F32)
            for i in range(MID * outer):
                acc[k, i // outer, i % outer] = mine[i * rows : (i + 1) * rows]
            return copy

        def stage2(k, copy):
            copy.wait_recv()
            for ai in range(outer):
                bsend[t, k, ai] = (acc[k, bp, ai] + crecv[t, k, bp, ai].astype(F32)).astype(BF16)
            copy = remote(
                bsend.at[t, k], brecv.at[t, k], b_sem.at[0, t, k], b_sem.at[1, t, k],
                tp=rank(a, bp, c),
            )
            copy.start()
            sends.append(copy)
            return copy

        def held(k, ai):
            return (
                acc[k, b, ai] + crecv[t, k, b, ai].astype(F32) + brecv[t, k, ai].astype(F32)
            )

        def stage3(k, copy):
            copy.wait_recv()
            copies = []
            for d, ai in enumerate(outer_peers):
                asend[t, k, d] = held(k, ai).astype(BF16)
                copy = remote(
                    asend.at[t, k, d], arecv.at[t, k, d],
                    a_send.at[t, k, d], a_recv.at[t, k, d], tp=rank(ai, b, c),
                )
                copy.start()
                sends.append(copy)
                copies.append(copy)
            return copies

        def stage4(k, copies):
            summed = held(k, a)
            for d, copy in enumerate(copies):
                copy.wait_recv()
                summed = summed + arecv[t, k, d].astype(F32)
            value = res[:, chunk(k)] + summed
            out[t, 0, :, chunk(k)] = value
            if t < WINDOW - 1:
                hsend[k] = value.astype(BF16)

                @pl.when(s < sections - 1)
                def _():
                    remote(
                        hsend.at[k], hrecv.at[k], h_sem.at[0, k], h_sem.at[1, k], section=s + 1
                    ).start()

        one, two, three = {}, {}, {}
        for step in range(CHUNKS + 3):
            if step < CHUNKS:
                one[step] = stage1(step)
            if 0 <= step - 1 < CHUNKS:
                two[step - 1] = stage2(step - 1, one[step - 1])
            if 0 <= step - 2 < CHUNKS:
                three[step - 2] = stage3(step - 2, two[step - 2])
            if 0 <= step - 3 < CHUNKS:
                stage4(step - 3, three[step - 3])

    for copy in sends:
        copy.wait_send()

    @pl.when(s < sections - 1)
    def _():
        for k in range(CHUNKS):
            remote(
                hsend.at[k], hrecv.at[k], h_sem.at[0, k], h_sem.at[1, k], section=s + 1
            ).wait_send()


def body(sections, ranks, states, text, visual, prefix, seg, gain, wq, wkv, wo):
    rows, depth = states.shape[1:]
    total = rows * ranks
    outer = ranks // (MID * INNER)
    cw = depth // CHUNKS
    qcols, kvcols = wq.shape[2], wkv.shape[2]
    hbm = pl.BlockSpec(memory_space=pl.ANY)
    dma = pltpu.SemaphoreType.DMA
    return pl.pallas_call(
        functools.partial(kernel, sections, ranks),
        out_shape=jax.ShapeDtypeStruct((WINDOW, 1, rows, depth), F32),
        in_specs=[hbm, hbm, hbm, pl.BlockSpec(memory_space=pltpu.SMEM)] + [hbm] * 5,
        out_specs=pl.BlockSpec(memory_space=pltpu.VMEM),
        scratch_shapes=[
            pltpu.VMEM((rows, depth), F32),
            pltpu.VMEM((rows, depth), BF16),
            pltpu.VMEM((rows, depth), BF16),
            pltpu.VMEM(seg.shape, jnp.int32),
            pltpu.VMEM((1, depth), F32),
            pltpu.VMEM((depth, qcols + kvcols), BF16),
            pltpu.VMEM((qcols, depth), BF16),
            pltpu.VMEM((rows, depth), F32),
            pltpu.VMEM((WINDOW, ranks, rows, depth), BF16),
            pltpu.VMEM((total, depth), BF16),
            pltpu.VMEM((INNER, total // INNER, qcols), BF16),
            pltpu.VMEM((CHUNKS, MID, outer, rows, cw), F32),
            pltpu.VMEM((WINDOW, CHUNKS, MID, outer, rows, cw), BF16),
            pltpu.VMEM((WINDOW, CHUNKS, MID, outer, rows, cw), BF16),
            pltpu.VMEM((WINDOW, CHUNKS, outer, rows, cw), BF16),
            pltpu.VMEM((WINDOW, CHUNKS, outer, rows, cw), BF16),
            pltpu.VMEM((WINDOW, CHUNKS, outer - 1, rows, cw), BF16),
            pltpu.VMEM((WINDOW, CHUNKS, outer - 1, rows, cw), BF16),
            pltpu.VMEM((CHUNKS, rows, cw), BF16),
            pltpu.VMEM((CHUNKS, rows, cw), BF16),
            dma((8,)),
            dma((WINDOW, ranks - 1)),
            dma((WINDOW, ranks)),
            dma((2, WINDOW, CHUNKS)),
            dma((2, WINDOW, CHUNKS)),
            dma((WINDOW, CHUNKS, outer - 1)),
            dma((WINDOW, CHUNKS, outer - 1)),
            dma((2, CHUNKS)),
        ],
        compiler_params=pltpu.CompilerParams(
            collective_id=0, has_side_effects=True, vmem_limit_bytes=56 * 1024 * 1024
        ),
        name="relay",
    )(states, text, visual, prefix, seg, gain, wq, wkv, wo)


def solution(mesh):
    sizes = dict(mesh.shape)
    return jax.shard_map(
        functools.partial(body, sizes["section"], sizes["tp"]),
        mesh=mesh,
        in_specs=(
            P("section", "tp", None),
            P(None, "tp", None),
            P(None, "tp", None),
            P(),
            P(),
            P("section", None),
            P("section", None, "tp"),
            P("section", None, "tp"),
            P("section", "tp", None),
        ),
        out_specs=P(None, "section", "tp", None),
        check_vma=False,
    )
```

time: 227 us -> 68.5 us (0.30)
  waiting for transfers between devices: 188 us -> 0 us
  Pallas kernels: 0 us -> 66.7 us
  between operations: 13.3 us -> 0.01 us
  other arithmetic: 11 us -> 0 us
  matrix products: 8.88 us -> 0 us
    reduce_scatter x2 -> x0, waiting for transfers between devices: 113 us -> none  [body(): lax.psum_scatter(jnp.dot(mixed_heads, out_w, preferred_element_type=jnp.f...]
    all_gather x2 -> x0, waiting for transfers between devices: 70.1 us -> none  [body(): normed = lax.all_gather(apply_normed, 'tp', axis=0, tiled=True)]
    pallas_call x0 -> x1, Pallas kernels: none -> 66.7 us  [body(): pl.pallas_call(functools.partial(kernel, sections, ranks), out_shape=jax....]
    dot_general x10 -> x0, matrix products: 8.39 us -> none  [the longest x2 3.66 us: body(): jnp.dot(normed, keyval_w, preferred_element_type=jnp.float32)]
    ppermute x1 -> x0, waiting for transfers between devices: 4.32 us -> none  [shifted(): return lax.ppermute(block, axis, route)]
    reduce_sum x6 -> x0, other arithmetic: 3.66 us -> none  [the longest x3 1.65 us: seg_offsets(): first_pos = jnp.sum(earlier, axis=1)]
    another operation x6 -> x0, other arithmetic: 2.67 us -> none  [the longest x2 2.35 us: body(): return jnp.stack(outputs)[:, None]]
    convert_element_type x4 -> x0, other arithmetic: 2.35 us -> none  [the longest x2 2.34 us: body(): apply_normed = rms_normed(residual, gain_row).astype(jnp.bfloat16)]
  transfers between devices with their start and end apart: 5 -> 0, of which waited for: 5 -> 0; matrix products, arithmetic and copies ran while one was open for 3% -> 0% of each run, Pallas kernels for 0% -> 0%
where the time goes in v1:
time: 68.5 us; the launch traced here: 68.3 us
  Pallas kernels  66.7 us (97%)
  local copies, waits for them, and re-layouts  1.67 us (2%)
    pallas_call x1, Pallas kernels, body(): pl.pallas_call(functools.partial(kernel, sections, ranks), out_shape=jax....  66.7 us
    unnamed x1, local copies, waits for them, and re-layouts  1.67 us

profile of v1, /device:TPU:6, one launch (start us, length us, event | category | flops | bytes accessed | tf_op | source)
XLA Modules:
  0.0 68.3 jit_solution(4070906696291265509)
XLA Ops:
  0.0 66.7 %relay.1 = f32[2,1,8,4096]{3,2,1,0:T(8,128)} custom-call(f32[1,8,4096]{2,1,0:T(8,128)} %states.1, bf16[1,8,4096]{2,1,0:T(8,128)(2,1)} %text.1, bf16[1,8,4096]{2,1,0:T(8,128)(2,1)} %visual.1, s32[1,4]{1,0:T(1,128)} %prefix.1, s32[3,128]{1,0:T(4,128)} %seg_in.1, f32[1,4096]{1,0:T(1,128)} %gain_in.1, bf16[1,4096,128]{2,1,0:T(8,128)(2,1)} %wq_in.1, ...), custom_call_target="tpu_custom_call" | custom-call | tf_op jit(solution)/shard_map/relay/pallas_call | solution.py:327
  66.7 1.7 %copy.11 = f32[2,1,8,4096]{3,2,1,0:T(8,128)} copy(f32[2,1,8,4096]{3,2,1,0:T(8,128)} %relay.1) | data formatting | bytes 524288

commit v2 on v1

--- a/solution.py
+++ b/solution.py
@@ -18,7 +18,10 @@
 
 MID = 2
 INNER = 2
-CHUNKS = 4
+CHUNKS = 8
+PIECES = 2
+LAG_ADD = 5
+LAG_MID = 3
 
 
 def iota(shape, dim):
@@ -46,6 +49,7 @@
     qcols = wq_in.shape[2]
     kvcols = wkv_in.shape[2]
     cw = depth // CHUNKS
+    pw = depth // PIECES
 
     def rank(ai, bi, ci):
         return (ai * MID + bi) * INNER + ci
@@ -66,7 +70,13 @@
     for load in loads:
         load.start()
 
-    outer_peers = [lax.rem(a + d, outer) for d in range(1, outer)]
+    if outer == 4:
+        flip = a + 1 - 2 * lax.rem(a, 2)
+        outer_peers = [flip, 3 - flip, 3 - a]
+        outer_from = outer_peers
+    else:
+        outer_peers = [lax.rem(a + d, outer) for d in range(1, outer)]
+        outer_from = [lax.rem(a - d + outer, outer) for d in range(1, outer)]
     tp_peers = [rank(ai, b, c) for ai in outer_peers] + [rank(a, bp, c), rank(a, b, cp)]
     barrier = pltpu.get_barrier_semaphore()
     for peer in tp_peers:
@@ -134,30 +144,35 @@
                     ).wait_recv()
                     res[:, k * cw : (k + 1) * cw] = hrecv[k].astype(F32)
 
-        xg[t, r] = normed(res[...])
+        mine = normed(res[...])
+        for p in range(PIECES):
+            xg[t, p, r] = mine[:, p * pw : (p + 1) * pw]
         if t == 0:
             beside = jnp.minimum(s, 1) + jnp.minimum(sections - 1 - s, 1)
             pl.semaphore_wait(barrier, len(tp_peers) + beside)
 
         used = [0]
 
-        def block(q, peer):
+        def block(p, q, peer):
             copy = remote(
-                xg.at[t, q], xg.at[t, q], ag_send.at[t, used[0]], ag_recv.at[t, q], tp=peer
+                xg.at[t, p, q], xg.at[t, p, q],
+                ag_send.at[t, used[0]], ag_recv.at[t, p, q], tp=peer,
             )
             used[0] += 1
             copy.start()
             sends.append(copy)
 
-        def arrived(q):
+        def arrived(p, q):
             remote(
-                xg.at[t, q], xg.at[t, q], ag_send.at[t, 0], ag_recv.at[t, q], tp=rank(a, b, cp)
+                xg.at[t, p, q], xg.at[t, p, q],
+                ag_send.at[t, 0], ag_recv.at[t, p, q], tp=rank(a, b, cp),
             ).wait_recv()
 
-        for ai in outer_peers:
-            block(r, rank(ai, b, c))
-        block(r, rank(a, bp, c))
-        block(r, rank(a, b, cp))
+        for p in range(PIECES):
+            block(p, r, rank(a, bp, c))
+            for ai in outer_peers:
+                block(p, r, rank(ai, b, c))
+            block(p, r, rank(a, b, cp))
 
         seg_here = seg_v[pl.ds(t - s + sections - 1, 1), :].astype(F32)
         seg_col = column_of(seg_here, total, 0)
@@ -171,28 +186,35 @@
         sine = jnp.where(front, -jnp.sin(angle), jnp.sin(angle))
         allowed = (seg_here == seg_col) & (iota((total, total), 1) <= iota((total, total), 0))
 
-        forward = [lax.rem(a - d + outer, outer) for d in range(1, outer)]
-        for ai in forward:
-            q = rank(ai, b, c)
-            arrived(q)
-            block(q, rank(a, bp, c))
-            block(q, rank(a, b, cp))
-        for ai in [a] + forward:
-            q = rank(ai, bp, c)
-            arrived(q)
-            block(q, rank(a, b, cp))
-        for ai in [a] + forward:
-            for bi in (b, bp):
-                arrived(rank(ai, bi, cp))
-
-        for i in range(ranks // 2):
-            xf[i * 2 * rows : (i + 1) * 2 * rows, :] = jnp.concatenate(
-                [xg[t, 2 * i].astype(F32), xg[t, 2 * i + 1].astype(F32)], axis=0
-            ).astype(BF16)
+        hops = [(p, d) for p in range(PIECES) for d in range(outer)]
+        from_a = [a] + outer_from
+        for i in range(len(hops) + LAG_MID):
+            if i < len(hops) and hops[i][1] > 0:
+                p, d = hops[i]
+                q = rank(from_a[d], b, c)
+                arrived(p, q)
+                block(p, q, rank(a, bp, c))
+                block(p, q, rank(a, b, cp))
+            if i >= LAG_MID:
+                p, d = hops[i - LAG_MID]
+                q = rank(from_a[d], bp, c)
+                arrived(p, q)
+                block(p, q, rank(a, b, cp))
         if t == 0:
             loads[3].wait()
             loads[4].wait()
-        mapped = jnp.dot(xf[...], w_v[...], preferred_element_type=F32)
+        mapped = None
+        for p in range(PIECES):
+            for ai in from_a:
+                for bi in (b, bp):
+                    arrived(p, rank(ai, bi, cp))
+            cols = slice(p * pw, (p + 1) * pw)
+            for i in range(ranks // 2):
+                xf[i * 2 * rows : (i + 1) * 2 * rows, cols] = jnp.concatenate(
+                    [xg[t, p, 2 * i].astype(F32), xg[t, p, 2 * i + 1].astype(F32)], axis=0
+                ).astype(BF16)
+            part = jnp.dot(xf[:, cols], w_v[cols, :], preferred_element_type=F32)
+            mapped = part if mapped is None else mapped + part
 
         def rotate(value):
             swapped = jnp.where(
@@ -295,15 +317,16 @@
                     ).start()
 
         one, two, three = {}, {}, {}
-        for step in range(CHUNKS + 3):
-            if step < CHUNKS:
-                one[step] = stage1(step)
-            if 0 <= step - 1 < CHUNKS:
-                two[step - 1] = stage2(step - 1, one[step - 1])
-            if 0 <= step - 2 < CHUNKS:
-                three[step - 2] = stage3(step - 2, two[step - 2])
-            if 0 <= step - 3 < CHUNKS:
-                stage4(step - 3, three[step - 3])
+        for k in range(CHUNKS + 1):
+            if k < CHUNKS:
+                one[k] = stage1(k)
+            if k > 0:
+                two[k - 1] = stage2(k - 1, one[k - 1])
+        for k in range(CHUNKS + LAG_ADD):
+            if k < CHUNKS:
+                three[k] = stage3(k, two[k])
+            if k >= LAG_ADD:
+                stage4(k - LAG_ADD, three[k - LAG_ADD])
 
     for copy in sends:
         copy.wait_send()
@@ -338,7 +361,7 @@
             pltpu.VMEM((depth, qcols + kvcols), BF16),
             pltpu.VMEM((qcols, depth), BF16),
             pltpu.VMEM((rows, depth), F32),
-            pltpu.VMEM((WINDOW, ranks, rows, depth), BF16),
+            pltpu.VMEM((WINDOW, PIECES, ranks, rows, depth // PIECES), BF16),
             pltpu.VMEM((total, depth), BF16),
             pltpu.VMEM((INNER, total // INNER, qcols), BF16),
             pltpu.VMEM((CHUNKS, MID, outer, rows, cw), F32),
@@ -351,8 +374,8 @@
             pltpu.VMEM((CHUNKS, rows, cw), BF16),
             pltpu.VMEM((CHUNKS, rows, cw), BF16),
             dma((8,)),
-            dma((WINDOW, ranks - 1)),
-            dma((WINDOW, ranks)),
+            dma((WINDOW, PIECES * (ranks - 1))),
+            dma((WINDOW, PIECES, ranks)),
             dma((2, WINDOW, CHUNKS)),
             dma((2, WINDOW, CHUNKS)),
             dma((WINDOW, CHUNKS, outer - 1)),

time: 68.5 us -> 65.9 us (0.962); the launches traced: 68.3 us -> 64.9 us
  Pallas kernels: 66.7 us -> 63.2 us
    pallas_call x1, Pallas kernels: 66.7 us -> 63.2 us  [body(): pl.pallas_call(functools.partial(kernel, sections, ranks), out_shape=jax....]
where the time goes in v2:
time: 65.9 us; the launch traced here: 64.9 us
  Pallas kernels  63.2 us (96%)
  local copies, waits for them, and re-layouts  1.67 us (3%)
    pallas_call x1, Pallas kernels, body(): pl.pallas_call(functools.partial(kernel, sections, ranks), out_shape=jax....  63.2 us
    unnamed x1, local copies, waits for them, and re-layouts  1.67 us

profile of v2, /device:TPU:6, one launch (start us, length us, event | category | flops | bytes accessed | tf_op | source)
XLA Modules:
  0.0 64.9 jit_solution(4478383494111391201)
XLA Ops:
  0.0 63.2 %relay.1 = f32[2,1,8,4096]{3,2,1,0:T(8,128)} custom-call(f32[1,8,4096]{2,1,0:T(8,128)} %states.1, bf16[1,8,4096]{2,1,0:T(8,128)(2,1)} %text.1, bf16[1,8,4096]{2,1,0:T(8,128)(2,1)} %visual.1, s32[1,4]{1,0:T(1,128)} %prefix.1, s32[3,128]{1,0:T(4,128)} %seg_in.1, f32[1,4096]{1,0:T(1,128)} %gain_in.1, bf16[1,4096,128]{2,1,0:T(8,128)(2,1)} %wq_in.1, ...), custom_call_target="tpu_custom_call" | custom-call | tf_op jit(solution)/shard_map/relay/pallas_call | solution.py:350
  63.2 1.7 %copy.11 = f32[2,1,8,4096]{3,2,1,0:T(8,128)} copy(f32[2,1,8,4096]{3,2,1,0:T(8,128)} %relay.1) | data formatting | bytes 524288
